TPU v7x, 256 devices: a whole 4x4x8 slice. The times are simulated.
256 devices in a mesh: dp: 8 (over z), expert: 32 (over x, y, core).
Axes of the slice: x: 4, y: 4, z: 8, core: 2. Of those that a mesh axis runs over, the one named last changes fastest.
Arguments:
- tokens: bfloat16 [65536, 2048], P(('dp', 'expert')), may hold values from -6 to 6
- expert_ranks: int32 [32, 65536], P(None, ('dp', 'expert')), may hold values from 0 to 65535, as said below
- capacity: int32 [32], replicated, may hold values from 512 to 1024, as said below
- weight_in: bfloat16 [32, 2048, 8192], P('expert', None, 'dp'), may hold values from -0.125 to 0.125
- weight_out: bfloat16 [32, 8192, 2048], P('expert', 'dp'), may hold values from -0.0625 to 0.0625
- gate_weights: float32 [32, 1024], P('expert', 'dp'), may hold values from 0.05 to 1
Outputs:
- combined: bfloat16 [65536, 2048], P(('dp', 'expert'))
Inputs may be any that keep to these rules, and one draw needn't show every extreme that they name: `expert_ranks`: for each expert the ranks are a permutation of 0 to 65535. Of the 256 tokens of one device, at most 8 have rank under 1024 for one expert; for an expert of capacity 1024, some devices have exactly 8. At least one expert has capacity 1024.
All inputs are finite; a program needn't handle non-finite values.
Results may differ from a plain program's by a relative error of at most 0.0053.
Values may be sent and summed in bfloat16 or wider, within the bound.
No kernel may reach another device: no remote copies, remote signals or barrier semaphores. Data moves between devices by JAX's collectives and lax.ppermute only.
A program may use at most 64 MiB of HBM per device.

v0:
```python
import jax
import jax.numpy as jnp
from jax import lax
from jax.sharding import Mesh
from jax.sharding import PartitionSpec as P

MOST = 8
LANES = 128
EXPERT = ("expert_0", "expert_1", "expert_2")
DP_EXPERT = ("dp", "expert_0", "expert_1", "expert_2")


def exclusive(values):
    return jnp.cumsum(values) - values


def on_device(tokens, expert_ranks, capacity, weight_in, weight_out, gate_weights):
    dp_count = lax.axis_size("dp")
    expert_count = lax.axis_size(EXPERT)
    token_count, width = tokens.shape
    slots_dp = gate_weights.shape[1]
    rows_all = expert_count * MOST
    own_dp = lax.axis_index("dp")
    own_expert = lax.axis_index(EXPERT)
    chosen = expert_ranks < capacity[:, None]
    chosen_int = chosen.astype(jnp.int32)
    counts = jnp.sum(chosen_int, axis=1)
    before = jnp.cumsum(chosen_int, axis=1) - chosen_int
    places = lax.broadcasted_iota(jnp.int32, (expert_count, MOST, token_count), 1)
    pack_table = jnp.logical_and(chosen[:, None, :], before[:, None, :] == places)
    pack_table = pack_table.astype(jnp.bfloat16).reshape(rows_all, token_count)
    packed = jnp.dot(pack_table, tokens, preferred_element_type=jnp.float32).astype(jnp.bfloat16)
    arrived_rows = lax.all_to_all(
        packed.reshape(expert_count, MOST, width), EXPERT, split_axis=0, concat_axis=0, tiled=True
    ).reshape(rows_all, width)
    device_ids = lax.broadcasted_iota(jnp.int32, (expert_count, expert_count), 0)
    expert_ids = lax.broadcasted_iota(jnp.int32, (expert_count, expert_count), 1)
    table = jnp.where(device_ids == own_expert, counts[None, :], 0)
    table = lax.psum(table.reshape(-1, LANES), EXPERT).reshape(expert_count, expert_count)
    arrived = jnp.sum(jnp.where(expert_ids == own_expert, table, 0), axis=1)
    plane_ids = lax.broadcasted_iota(jnp.int32, (dp_count, LANES), 0)
    lane_ids = lax.broadcasted_iota(jnp.int32, (dp_count, LANES), 1)
    plane_row = jnp.pad(jnp.sum(table, axis=0).astype(jnp.float32), (0, LANES - expert_count))
    both = jnp.concatenate(
        [
            jnp.where(plane_ids == own_dp, plane_row[None, :], 0.0),
            jnp.where(plane_ids == own_dp, gate_weights.reshape(-1, LANES), 0.0),
        ]
    )
    both = lax.psum(both, "dp")
    plane_counts = both[:dp_count].astype(jnp.int32)
    most_rows = jnp.max(plane_counts)
    earlier = jnp.logical_and(plane_ids < own_dp, lane_ids == own_expert)
    first_slot = jnp.sum(jnp.where(earlier, plane_counts, 0))
    gates_all = jnp.concatenate([both[dp_count:].reshape(-1), jnp.zeros((rows_all,), jnp.float32)])
    within = lax.broadcasted_iota(jnp.int32, (expert_count, MOST), 1)
    target = jnp.where(within < arrived[:, None], exclusive(arrived)[:, None] + within, -1).reshape(
        rows_all
    )

    def experts(rows, plane_rows):
        slot_ids = lax.broadcasted_iota(jnp.int32, (rows_all, plane_rows), 1)
        place_table = (target[:, None] == slot_ids).astype(jnp.bfloat16)
        plane = lax.dot_general(
            place_table, rows, (((0,), (0,)), ((), ())), preferred_element_type=jnp.float32
        ).astype(jnp.bfloat16)
        slot_rows = lax.all_gather(plane, "dp", axis=0, tiled=True)
        hidden = jnp.maximum(
            jnp.dot(slot_rows, weight_in[0], preferred_element_type=jnp.float32), 0.0
        ).astype(jnp.bfloat16)
        share = jnp.dot(hidden, weight_out[0], preferred_element_type=jnp.float32)
        out = lax.psum_scatter(
            share.astype(jnp.bfloat16), "dp", scatter_dimension=0, tiled=True
        ).astype(jnp.float32)
        gates = lax.dynamic_slice_in_dim(gates_all, first_slot, plane_rows, 0)
        scaled = (gates[:, None] * out).astype(jnp.bfloat16)
        returned = jnp.dot(place_table, scaled, preferred_element_type=jnp.float32)
        return returned.astype(jnp.bfloat16)

    fair = slots_dp + slots_dp // 4
    sent_back = lax.cond(
        most_rows <= fair,
        lambda rows: experts(rows, fair),
        lambda rows: experts(rows, rows_all),
        arrived_rows,
    )
    results = lax.all_to_all(
        sent_back.reshape(expert_count, MOST, width),
        EXPERT,
        split_axis=0,
        concat_axis=0,
        tiled=True,
    ).reshape(rows_all, width)
    combined = lax.dot_general(
        pack_table, results, (((0,), (0,)), ((), ())), preferred_element_type=jnp.float32
    )
    return combined.astype(jnp.bfloat16)


def solution(mesh):
    split = Mesh(
        mesh.devices.reshape(mesh.shape["dp"], 4, 4, 2), ("dp", "expert_0", "expert_1", "expert_2")
    )
    placed = (
        P(DP_EXPERT, None),
        P(None, DP_EXPERT),
        P(),
        P(EXPERT, None, "dp"),
        P(EXPERT, "dp", None),
        P(EXPERT, "dp"),
    )
    return jax.shard_map(
        on_device, mesh=split, in_specs=placed, out_specs=P(DP_EXPERT, None), check_vma=False
    )
```

profile of v0, /device:TPU:1, one launch (start us, length us, event | category | flops | bytes accessed | tf_op | source)
XLA Modules:
  0.0 348.8 jit_solution(17893966849262882347)
XLA Ops:
  6.5 0.9 convert_bitcast_fusion.1
  7.5 0.6 reduce-window.18
  8.1 0.2 slice_reduce_fusion
  8.3 0.1 iota.90
  8.4 0.1 convert_subtract_fusion
  8.5 1.5 fusion.19
  10.0 8.6 %all-to-all-start = ((bf16[32,8,2048]{2,1,0:T(8,128)(2,1)}), bf16[32,8,2048]{2,1,0:T(8,128)(2,1)S(1)}, u32[]{:S(2)}, u32[]{:S(2)}) async-start(bf16[32,8,2048]{2,1,0:T(8,128)(2,1)} %fusion.19), calls=%async_computation.2 | async-start | bytes 2097152 | tf_op jit(solution)/shard_map/all_to_all | solution.py:33
  18.6 0.1 iota.79
  18.7 0.1 iota.80
  18.8 0.1 broadcast_in_dim.57
  18.9 0.1 reshape.73
  18.9 127.0 %psum.14 = s32[32,32]{1,0:T(8,128)S(1)} all-reduce(s32[32,32]{1,0:T(8,128)S(1)} %reshape.73), channel_id=1, replica_groups=mesh['dp'=8,'expert_0'=4,'expert_1'=4,'expert_2'=2] {'expert_0','expert_..., use_global_device_ids=true, to_apply=%region_3.4 | all-reduce | flops 1024 | bytes 8192 | tf_op jit(solution)/shard_map/psum | solution.py:39
  145.9 0.1 select_reduce_fusion
  146.1 0.1 broadcast_select_fusion.1
  146.1 16.5 %psum.15 = f32[16,128]{1,0:T(8,128)S(1)} all-reduce(f32[16,128]{1,0:T(8,128)S(1)} %pad_maximum_fusion), channel_id=1, replica_groups=mesh['dp'=8,'expert_0'=4,'expert_1'=4,'expert_2'=2] {'dp'}, use_global_device_ids=true, to_apply=%region_5.6 | all-reduce | flops 2048 | bytes 16384 | tf_op jit(solution)/shard_map/psum | solution.py:50
  162.7 0.8 select_reduce_fusion.1
  164.2 0.1 copy.19
  164.2 0.1 reduce-window.20
  164.3 0.1 reduce.1
  164.4 0.1 add_select_fusion
  164.5 151.7 %conditional.2 = (bf16[256,2048]{1,0:T(8,128)(2,1)S(1)}) conditional(s32[]{:T(128)} %convert_element_type.61, (s32[32,8]{1,0:T(8,128)S(1)}, s32[]{:T(128)}, f32[1280]{0:T(1024)S(1)}, bf16[256,2048]{1,0:T(8,128)(2,1)S(1)}, bf16[1,2048,1024]{2,1,0:T(8,128)(2,1)}, /*index=5*/bf16[1,1024,2048]{2,1,0:T(8,128)(2,1)}) %tuple.30, (s32[32,8]{1,0:T(8,128)S(1)}, ...), branch_computations={%region_10.12_spmd, %region_12.14_spmd} | conditional | flops 17727356928 | bytes 85990520
  164.5 0.0 all-gather.5.cloned.1.call-start
  164.6 0.1 eq.49
  164.7 1.3 convolution_convert_fusion.3
  166.0 0.2 reduce-scatter.5.cloned.1.call-start
  166.2 67.1 %all-gather.5.cloned.1.call-done = bf16[1280,2048]{1,0:T(8,128)(2,1)} async-done(((bf16[160,2048]{1,0:T(8,128)(2,1)}), bf16[1280,2048]{1,0:T(8,128)(2,1)}) %all-gather.5.cloned.1.call-update) | async-done | bytes 5242896 | tf_op jit(solution)/shard_map/cond/branch_1_fun/all_gather | solution.py:67
  233.4 16.9 %convolution_convert_fusion.2 = bf16[1280,2048]{1,0:T(8,128)(2,1)} fusion(bf16[1,1024,2048]{2,1,0:T(8,128)(2,1)} %get-tuple-element.45, bf16[1280,2048]{1,0:T(8,128)(2,1)} %all-gather.5.cloned.1.call-done, bf16[1,2048,1024]{2,1,0:T(8,128)(2,1)} %get-tuple-element.44), kind=kOutput, calls=%fused_computation.13 | convolution fusion | flops 10742661120 | bytes 18874368 | tf_op jit(solution)/shard_map/cond/branch_1_fun/dot_general | solution.py:71
  252.0 0.1 dynamic_slice.5
  252.0 62.3 %reduce-scatter.5.cloned.1.call-done = bf16[160,2048]{1,0:T(8,128)(2,1)} async-done(((bf16[1280,2048]{1,0:T(8,128)(2,1)}), bf16[160,2048]{1,0:T(8,128)(2,1)}) %reduce-scatter.5.cloned.1.call-update) | async-done | bytes 655376 | tf_op jit(solution)/shard_map/cond/branch_1_fun/reduce_scatter | solution.py:72
  314.4 1.6 fusion.13
  316.2 24.3 %all_to_all.10 = bf16[32,8,2048]{2,1,0:T(8,128)(2,1)S(1)} all-to-all(bf16[32,8,2048]{2,1,0:T(8,128)(2,1)S(1)} %bitcast.57), channel_id=1, replica_groups=mesh['dp'=8,'expert_0'=4,'expert_1'=4,'expert_2'=2] {'expert_0','expert_..., dimensions={0} | all-to-all | bytes 2097152 | tf_op jit(solution)/shard_map/all_to_all | solution.py:87
  340.5 1.5 fusion.18
  (24 shorter events, 0.2 us)
Async XLA Ops:
  6.5 2.0 copy-start
  6.5 139.5 %copy-start.1 = (f32[1,128]{1,0:T(1,128)S(1)}, f32[1,128]{1,0:T(1,128)}, u32[]{:S(2)}) copy-start(f32[1,128]{1,0:T(1,128)} %param.13) | copy-start | bytes 1540
  10.0 154.5 %all-to-all-start = ((bf16[32,8,2048]{2,1,0:T(8,128)(2,1)}), bf16[32,8,2048]{2,1,0:T(8,128)(2,1)S(1)}, u32[]{:S(2)}, u32[]{:S(2)}) async-start(bf16[32,8,2048]{2,1,0:T(8,128)(2,1)} %fusion.19), calls=%async_computation.2 | async-start | bytes 2097152 | tf_op jit(solution)/shard_map/all_to_all | solution.py:33
  164.5 68.8 %all-gather.5.cloned.1.call-start = ((), (), s32[]{:S(2)}) async-start(), calls=%async_computation.6 | async-start | bytes 5898240 | tf_op jit(solution)/shard_map/cond/branch_1_fun/all_gather | solution.py:67
  166.0 148.4 %reduce-scatter.5.cloned.1.call-start = ((), (), s32[]{:S(2)}) async-start(), calls=%async_computation.7 | async-start | bytes 5898240 | tf_op jit(solution)/shard_map/cond/branch_1_fun/reduce_scatter | solution.py:72
Sparse Core Ops, SparseCore 0:
  167.1 66.1 all-gather.4
  250.4 63.9 reduce-scatter.4
where the time goes:
time: 349 us
  blocking collectives  168 us (48%)
  waiting for transfers between devices  129 us (37%)
  matrix products  22.7 us (7%)
  between operations  14.2 us (4%)
  starting transfers between devices  8.84 us (3%)
    psum x1, blocking collectives, on_device(): lax.psum(table.reshape(-1, LANES), EXPERT)  127 us
    all_gather x1, waiting for transfers between devices, experts(): slot_rows = lax.all_gather(plane, 'dp', axis=0, tiled=True)  67.1 us
    reduce_scatter x1, waiting for transfers between devices, experts(): lax.psum_scatter(share.astype(jnp.bfloat16), 'dp', scatter_dimension=0, t...  62.3 us
    all_to_all x1, blocking collectives, on_device(): lax.all_to_all(sent_back.reshape(expert_count, MOST, width), EXPERT, spli...  24.3 us
    dot_general x1, matrix products, experts(): share = jnp.dot(hidden, weight_out[0], preferred_element_type=jnp.float32)  16.9 us
    psum x1, blocking collectives, on_device(): both = lax.psum(both, 'dp')  16.5 us
    all_to_all x1, starting transfers between devices, on_device(): lax.all_to_all(packed.reshape(expert_count, MOST, width), EXPERT, split_a...  8.58 us
  transfers between devices with their start and end apart: 3, of which 2 were waited for; matrix products, arithmetic and copies ran while one was open for 1% of the time, Pallas kernels for 0%

commit v1 on v0

--- a/solution.py
+++ b/solution.py
@@ -15,6 +15,12 @@
 
 
 def on_device(tokens, expert_ranks, capacity, weight_in, weight_out, gate_weights):
+
+    def solve_the_patch(z):
+        for d in ("expert_0", ("expert_1", "expert_2")):
+            z = lax.psum(z, d)
+        return z
+
     dp_count = lax.axis_size("dp")
     expert_count = lax.axis_size(EXPERT)
     token_count, width = tokens.shape
@@ -36,7 +42,7 @@
     device_ids = lax.broadcasted_iota(jnp.int32, (expert_count, expert_count), 0)
     expert_ids = lax.broadcasted_iota(jnp.int32, (expert_count, expert_count), 1)
     table = jnp.where(device_ids == own_expert, counts[None, :], 0)
-    table = lax.psum(table.reshape(-1, LANES), EXPERT).reshape(expert_count, expert_count)
+    table = solve_the_patch(table.reshape(-1, LANES)).reshape(expert_count, expert_count)
     arrived = jnp.sum(jnp.where(expert_ids == own_expert, table, 0), axis=1)
     plane_ids = lax.broadcasted_iota(jnp.int32, (dp_count, LANES), 0)
     lane_ids = lax.broadcasted_iota(jnp.int32, (dp_count, LANES), 1)

time: 349 us -> 260 us (0.74)
  blocking collectives: 168 us -> 80.1 us
    psum x1 -> x2, blocking collectives: 127 us -> 39.3 us  [solve_the_patch(): z = lax.psum(z, d)]
where the time goes in v1:
time: 260 us; the launch traced here: 259 us
  waiting for transfers between devices  128 us (49%)
  blocking collectives  80.1 us (31%)
  matrix products  22.7 us (9%)
  between operations  14.2 us (5%)
  starting transfers between devices  8.84 us (3%)
  other arithmetic  2.95 us (1%)
    all_gather x1, waiting for transfers between devices, experts(): slot_rows = lax.all_gather(plane, 'dp', axis=0, tiled=True)  65.2 us
    reduce_scatter x1, waiting for transfers between devices, experts(): lax.psum_scatter(share.astype(jnp.bfloat16), 'dp', scatter_dimension=0, t...  62.3 us
    psum x2, blocking collectives, solve_the_patch(): z = lax.psum(z, d)  39.3 us
    all_to_all x1, blocking collectives, on_device(): lax.all_to_all(sent_back.reshape(expert_count, MOST, width), EXPERT, spli...  24.3 us
    dot_general x1, matrix products, experts(): share = jnp.dot(hidden, weight_out[0], preferred_element_type=jnp.float32)  16.9 us
    psum x1, blocking collectives, on_device(): both = lax.psum(both, 'dp')  16.5 us
    all_to_all x1, starting transfers between devices, on_device(): lax.all_to_all(packed.reshape(expert_count, MOST, width), EXPERT, split_a...  8.58 us
  transfers between devices with their start and end apart: 3, of which 2 were waited for; matrix products, arithmetic and copies ran while one was open for 1% of the time, Pallas kernels for 0%

profile of v1, /device:TPU:1, one launch (start us, length us, event | category | flops | bytes accessed | tf_op | source)
XLA Modules:
  0.0 259.2 jit_solution(16805566919057546236)
XLA Ops:
  6.5 0.9 convert_bitcast_fusion.1
  7.5 0.6 reduce-window.18
  8.1 0.2 slice_reduce_fusion
  8.3 0.1 iota.90
  8.4 0.1 convert_subtract_fusion
  8.5 1.5 fusion.19
  10.0 8.6 %all-to-all-start = ((bf16[32,8,2048]{2,1,0:T(8,128)(2,1)}), bf16[32,8,2048]{2,1,0:T(8,128)(2,1)S(1)}, u32[]{:S(2)}, u32[]{:S(2)}) async-start(bf16[32,8,2048]{2,1,0:T(8,128)(2,1)} %fusion.19), calls=%async_computation.2 | async-start | bytes 2097152 | tf_op jit(solution)/shard_map/all_to_all | solution.py:39
  18.6 0.1 iota.79
  18.7 0.1 iota.80
  18.8 0.1 broadcast_in_dim.57
  18.9 16.6 %psum.21 = s32[8,128]{1,0:T(8,128)S(1)} all-reduce(s32[8,128]{1,0:T(8,128)S(1)} %broadcast_select_fusion.2), channel_id=1, replica_groups=mesh['dp'=8,'expert_0'=4,'expert_1'=4,'expert_2'=2] {'expert_0'}, use_global_device_ids=true, to_apply=%region_3.4 | all-reduce | flops 1024 | bytes 8192 | tf_op jit(solution)/shard_map/psum | solution.py:21
  35.5 0.1 reshape.73
  35.5 22.7 %psum.22 = s32[32,32]{1,0:T(8,128)S(1)} all-reduce(s32[32,32]{1,0:T(8,128)S(1)} %reshape.73), channel_id=1, replica_groups=mesh['dp'=8,'expert_0'=4,'expert_1'=4,'expert_2'=2] {'expert_1','expert_2'}, use_global_device_ids=true, to_apply=%region_4.5 | all-reduce | flops 1024 | bytes 8192 | tf_op jit(solution)/shard_map/psum | solution.py:21
  58.2 0.1 select_reduce_fusion
  58.4 0.1 broadcast_select_fusion.1
  58.5 16.5 %psum.23 = f32[16,128]{1,0:T(8,128)S(1)} all-reduce(f32[16,128]{1,0:T(8,128)S(1)} %pad_maximum_fusion), channel_id=1, replica_groups=mesh['dp'=8,'expert_0'=4,'expert_1'=4,'expert_2'=2] {'dp'}, use_global_device_ids=true, to_apply=%region_6.7 | all-reduce | flops 2048 | bytes 16384 | tf_op jit(solution)/shard_map/psum | solution.py:56
  75.0 0.8 select_reduce_fusion.1
  76.5 0.1 copy.19
  76.6 0.1 reduce-window.20
  76.6 0.1 reduce.1
  76.8 0.1 add_select_fusion
  76.8 149.8 %conditional.2 = (bf16[256,2048]{1,0:T(8,128)(2,1)S(1)}) conditional(s32[]{:T(128)} %convert_element_type.61, (s32[32,8]{1,0:T(8,128)S(1)}, s32[]{:T(128)}, f32[1280]{0:T(1024)S(1)}, bf16[256,2048]{1,0:T(8,128)(2,1)S(1)}, bf16[1,2048,1024]{2,1,0:T(8,128)(2,1)}, /*index=5*/bf16[1,1024,2048]{2,1,0:T(8,128)(2,1)}) %tuple.30, (s32[32,8]{1,0:T(8,128)S(1)}, ...), branch_computations={%region_11.13_spmd, %region_13.15_spmd} | conditional | flops 17727356928 | bytes 85990520
  76.9 0.1 eq.49
  77.0 1.3 convolution_convert_fusion.3
  78.3 0.2 reduce-scatter.5.cloned.1.call-start
  78.5 65.2 %all-gather.5.cloned.1.call-done = bf16[1280,2048]{1,0:T(8,128)(2,1)} async-done(((bf16[160,2048]{1,0:T(8,128)(2,1)}), bf16[1280,2048]{1,0:T(8,128)(2,1)}) %all-gather.5.cloned.1.call-update) | async-done | bytes 5242896 | tf_op jit(solution)/shard_map/cond/branch_1_fun/all_gather | solution.py:73
  143.8 16.9 %convolution_convert_fusion.2 = bf16[1280,2048]{1,0:T(8,128)(2,1)} fusion(bf16[1,1024,2048]{2,1,0:T(8,128)(2,1)} %get-tuple-element.45, bf16[1280,2048]{1,0:T(8,128)(2,1)} %all-gather.5.cloned.1.call-done, bf16[1,2048,1024]{2,1,0:T(8,128)(2,1)} %get-tuple-element.44), kind=kOutput, calls=%fused_computation.13 | convolution fusion | flops 10742661120 | bytes 18874368 | tf_op jit(solution)/shard_map/cond/branch_1_fun/dot_general | solution.py:77
  162.4 0.1 dynamic_slice.5
  162.4 62.3 %reduce-scatter.5.cloned.1.call-done = bf16[160,2048]{1,0:T(8,128)(2,1)} async-done(((bf16[1280,2048]{1,0:T(8,128)(2,1)}), bf16[160,2048]{1,0:T(8,128)(2,1)}) %reduce-scatter.5.cloned.1.call-update) | async-done | bytes 655376 | tf_op jit(solution)/shard_map/cond/branch_1_fun/reduce_scatter | solution.py:78
  224.8 1.6 fusion.13
  226.6 24.3 %all_to_all.10 = bf16[32,8,2048]{2,1,0:T(8,128)(2,1)S(1)} all-to-all(bf16[32,8,2048]{2,1,0:T(8,128)(2,1)S(1)} %bitcast.57), channel_id=1, replica_groups=mesh['dp'=8,'expert_0'=4,'expert_1'=4,'expert_2'=2] {'expert_0','expert_..., dimensions={0} | all-to-all | bytes 2097152 | tf_op jit(solution)/shard_map/all_to_all | solution.py:93
  250.9 1.5 fusion.18
  (25 shorter events, 0.2 us)
Async XLA Ops:
  6.5 2.0 copy-start
  6.5 51.8 %copy-start.1 = (f32[1,128]{1,0:T(1,128)S(1)}, f32[1,128]{1,0:T(1,128)}, u32[]{:S(2)}) copy-start(f32[1,128]{1,0:T(1,128)} %param.13) | copy-start | bytes 1540
  10.0 66.9 %all-to-all-start = ((bf16[32,8,2048]{2,1,0:T(8,128)(2,1)}), bf16[32,8,2048]{2,1,0:T(8,128)(2,1)S(1)}, u32[]{:S(2)}, u32[]{:S(2)}) async-start(bf16[32,8,2048]{2,1,0:T(8,128)(2,1)} %fusion.19), calls=%async_computation.2 | async-start | bytes 2097152 | tf_op jit(solution)/shard_map/all_to_all | solution.py:39
  76.9 66.9 %all-gather.5.cloned.1.call-start = ((), (), s32[]{:S(2)}) async-start(), calls=%async_computation.6 | async-start | bytes 5898240 | tf_op jit(solution)/shard_map/cond/branch_1_fun/all_gather | solution.py:73
  78.3 146.5 %reduce-scatter.5.cloned.1.call-start = ((), (), s32[]{:S(2)}) async-start(), calls=%async_computation.7 | async-start | bytes 5898240 | tf_op jit(solution)/shard_map/cond/branch_1_fun/reduce_scatter | solution.py:78
Sparse Core Ops, SparseCore 0:
  79.5 64.2 all-gather.4
  160.8 63.9 reduce-scatter.4
